TPU v7x, 32 devices: a whole 2x2x4 slice. The times are simulated.
32 devices in a mesh: ctx: 8 (over z, x), tp: 4 (over y, core).
Axes of the slice: x: 2, y: 2, z: 4, core: 2. Of those that a mesh axis runs over, the one named last changes fastest.
Arguments:
- queries: bfloat16 [2048, 8192], P('ctx', 'tp'), may hold values from -8 to 8
- keys: bfloat16 [2048, 1024], P('ctx'), may hold values from -7 to 7
- values: bfloat16 [2048, 1024], P('ctx'), may hold values from -6 to 6
- out_weight: bfloat16 [8192, 4096], P('tp'), may hold values from -0.25 to 0.25
- block_order: int32 [16], P('ctx'), may hold values from 0 to 15, each once
Outputs:
- projected: bfloat16 [2048, 4096], P('ctx', 'tp')
Inputs may be any that keep to these rules, and one draw needn't show every extreme that they name: `block_order`: every sequence block appears exactly once.
All inputs are finite; a program needn't handle non-finite values.
Results may differ from a plain program's by a relative error of at most 0.015.
Values may be sent and summed in bfloat16 or wider, within the bound.
A program may use at most 64 MiB of HBM per device.

v0:
```python
import math
import jax
import jax.numpy as jnp
from jax import lax
from jax.sharding import PartitionSpec as P

QUERY_HEADS = 64
KEY_VALUE_HEADS = 8
HEAD_SIZE = 128


def shards(queries, keys, values, out_weight, block_order):
    tok_rows = queries.shape[0]
    block_len = tok_rows // 2
    heads_dev = queries.shape[1] // HEAD_SIZE
    group_size = QUERY_HEADS // KEY_VALUE_HEADS
    kv_heads = max(1, heads_dev // group_size)
    head_group = heads_dev // kv_heads
    whole_order = lax.all_gather(block_order, "ctx", axis=0, tiled=True)
    offsets = jnp.arange(block_len, dtype=jnp.int32)
    all_pos = (whole_order[:, None] * block_len + offsets[None, :]).reshape(-1)
    local_pos = (block_order[:, None] * block_len + offsets[None, :]).reshape(-1)
    first_head = lax.axis_index("tp") * heads_dev // group_size
    column_start = first_head * HEAD_SIZE
    own_keys = lax.dynamic_slice_in_dim(keys, column_start, kv_heads * HEAD_SIZE, 1)
    own_values = lax.dynamic_slice_in_dim(values, column_start, kv_heads * HEAD_SIZE, 1)
    scale = 1.0 / math.sqrt(HEAD_SIZE)
    query_heads = queries.reshape(tok_rows, kv_heads, head_group, HEAD_SIZE)
    last_pos = jnp.max(local_pos)

    def update(state, key_block, value_block, pos_block):
        run_max, run_sum, accum = state
        keyed = key_block.reshape(-1, kv_heads, HEAD_SIZE)
        valued = value_block.reshape(-1, kv_heads, HEAD_SIZE)
        scores = (
            jnp.einsum("tkgd,skd->kgts", query_heads, keyed, preferred_element_type=jnp.float32)
            * scale
        )
        visible = pos_block[None, None, None, :] <= local_pos[None, None, :, None]
        new_max = jnp.maximum(run_max, jnp.max(jnp.where(visible, scores, -1e30), axis=-1))
        weights = jnp.where(visible, jnp.exp(scores - new_max[..., None]), 0.0)
        factor = jnp.exp(run_max - new_max)
        run_sum = run_sum * factor + jnp.sum(weights, axis=-1)
        spread = jnp.transpose(factor, (2, 0, 1))[..., None]
        accum = accum * spread + jnp.einsum(
            "kgts,skd->tkgd",
            weights.astype(jnp.bfloat16),
            valued,
            preferred_element_type=jnp.float32,
        )
        return (new_max, run_sum, accum)

    start_state = (
        jnp.full((kv_heads, head_group, tok_rows), -1e30, jnp.float32),
        jnp.zeros((kv_heads, head_group, tok_rows), jnp.float32),
        jnp.zeros((tok_rows, kv_heads, head_group, HEAD_SIZE), jnp.float32),
    )
    piece_keys = lax.all_gather(own_keys, "ctx", axis=0, tiled=True)
    piece_values = lax.all_gather(own_values, "ctx", axis=0, tiled=True)
    rows = piece_keys.shape[0]
    step_rows = math.gcd(rows, 512)

    def advance(carry, blocks):
        result = lax.cond(
            jnp.min(blocks[2]) <= last_pos,
            lambda inner: update(inner, blocks[0], blocks[1], blocks[2]),
            lambda inner: inner,
            carry,
        )
        return (result, None)

    stacked = (
        piece_keys.reshape(rows // step_rows, step_rows, -1),
        piece_values.reshape(rows // step_rows, step_rows, -1),
        all_pos.reshape(rows // step_rows, step_rows),
    )
    result, _ = lax.scan(advance, start_state, stacked)
    run_max, run_sum, accum = result
    totals = jnp.transpose(run_sum, (2, 0, 1))[..., None]
    attended = (accum / totals).reshape(tok_rows, heads_dev * HEAD_SIZE).astype(jnp.bfloat16)
    summed = lax.psum_scatter(
        lax.dot_general(
            out_weight, attended, (((0,), (1,)), ((), ())), preferred_element_type=jnp.float32
        ).astype(jnp.bfloat16),
        "tp",
        scatter_dimension=0,
        tiled=True,
    ).astype(jnp.float32)
    return summed.T.astype(jnp.bfloat16)


def solution(mesh):
    in_specs = (P("ctx", "tp"), P("ctx", None), P("ctx", None), P("tp", None), P("ctx"))
    out_specs = P("ctx", "tp")
    return jax.shard_map(shards, mesh=mesh, in_specs=in_specs, out_specs=out_specs, check_vma=False)
```

profile of v0, /device:TPU:0, one launch (start us, length us, event | category | flops | bytes accessed | tf_op | source)
XLA Modules:
  0.0 189.9 jit_solution(12870223693085715618)
XLA Ops:
  6.5 1.0 copy-done
  7.6 0.7 constant_dynamic-slice_fusion.4
  8.3 1.6 constant_dynamic-slice_fusion.3
  10.0 1.3 dynamic-slice
  12.0 0.9 dynamic-update-slice
  12.8 13.1 %all-reduce = s32[16]{0:T(128)S(1)} all-reduce(s32[16]{0:T(128)S(1)} %dynamic-update-slice), channel_id=1, replica_groups=mesh['ctx'=8,'tp'=4] {'ctx'}, use_global_device_ids=true, to_apply=%add | all-reduce | flops 16 | bytes 128
  26.1 1.5 copy.24
  27.5 0.7 copy.26
  28.2 0.7 broadcast_multiply_fusion
  28.9 0.7 add_reduce_fusion
  29.7 22.8 %all-gather.3.cloned.1.call-done = bf16[2048,256]{1,0:T(8,128)(2,1)} async-done(((bf16[256,256]{1,0:T(8,128)(2,1)}), bf16[2048,256]{1,0:T(8,128)(2,1)}) %all-gather.3.cloned.1.call-update) | async-done | bytes 1048592 | tf_op jit(solution)/shard_map/all_gather | solution.py:58
  52.5 1.5 copy.25
  54.0 39.6 %all-gather.5.cloned.1.call-done = bf16[2048,256]{1,0:T(8,128)(2,1)} async-done(((bf16[256,256]{1,0:T(8,128)(2,1)}), bf16[2048,256]{1,0:T(8,128)(2,1)}) %all-gather.5.cloned.1.call-update) | async-done | bytes 1048592 | tf_op jit(solution)/shard_map/all_gather | solution.py:59
  93.7 2.3 %copy.27 = bf16[4,512,256]{1,2,0:T(8,128)(2,1)} copy(bf16[4,512,256]{2,1,0:T(8,128)(2,1)} %bitcast.58) | data formatting | bytes 2097152
  95.9 1.6 broadcast_in_dim.44
  97.5 43.6 %while.15 = (s32[]{:T(128)}, f32[2,8,256]{2,1,0:T(8,128)S(1)}, f32[2,8,256]{2,1,0:T(8,128)S(1)}, f32[256,2,8,128]{3,0,2,1:T(8,128)}, s32[4,512]{1,0:T(4,128)S(1)...) while((s32[]{:T(128)}, f32[2,8,256]{2,1,0:T(8,128)S(1)}, ...), condition=%wide.region_7.8_spmd.clone, body=%wide.region_1.7_spmd.clone.sunk | while | flops 1098003200 | bytes 49555792 | solution.py:77
  97.5 0.6 fusion.23
  99.4 9.0 %conditional.3 = ((f32[2,8,256]{2,1,0:T(8,128)S(1)}, f32[2,8,256]{2,1,0:T(8,128)S(1)}, f32[256,2,8,128]{3,0,2,1:T(8,128)})) conditional(s32[]{:T(128)} %convert_element_type.40, (f32[2,8,256]{2,1,0:T(8,128)S(1)}, f32[2,8,256]{2,1,0:T(8,128)S(1)}, f32[256,2,8,128]{3,0,2,1:T(8,128)}) %tuple.45, (s32[1,512]{1,0:T(1,128)S(1)}, s32[2]{0:T(128)S(1)}, ...), branch_computations={%region_3.3_spmd, %region_4.6_spmd} | conditional | flops 1098002688 | bytes 49550436 | solution.py:64
  99.6 1.0 constant_dynamic-slice_fusion
  100.6 1.5 fusion.2
  102.2 1.7 fusion.6
  103.9 3.2 %bitcast_add_fusion = f32[256,2,8,128]{3,0,2,1:T(8,128)S(1)} fusion(f32[256,2,8,128]{3,0,2,1:T(8,128)S(1)} %copy-done.1, bf16[512,2,128,1]{0,2,3,1:T(8,128)(2,1)S(1)} %bitcast.54, f32[2,512,256,8]{2,1,3,0:T(8,128)S(1)} %get-tuple-element.228, f32[2,8,256]{2,1,0:T(8,128)S(1)} %get-tuple-element.305, pred[256,512]{0,1:T(8,128)(4,1)S(1)} %broadcast_compare_fusion, ...), kind=kOutput, calls=%fused_computation.10 | convolution fusion | flops 546308096 | bytes 13008896 | tf_op jit(solution)/shard_map/while/body/eval_jaxpr/cond/branch_1_fun/kgts,skd->tkgd/dot_general | solution.py:45
  107.1 1.3 copy-done.2
  108.4 0.6 fusion.23
  110.3 9.0 %conditional.3 = ((f32[2,8,256]{2,1,0:T(8,128)S(1)}, f32[2,8,256]{2,1,0:T(8,128)S(1)}, f32[256,2,8,128]{3,0,2,1:T(8,128)})) conditional(s32[]{:T(128)} %convert_element_type.40, (f32[2,8,256]{2,1,0:T(8,128)S(1)}, f32[2,8,256]{2,1,0:T(8,128)S(1)}, f32[256,2,8,128]{3,0,2,1:T(8,128)}) %tuple.45, (s32[1,512]{1,0:T(1,128)S(1)}, s32[2]{0:T(128)S(1)}, ...), branch_computations={%region_3.3_spmd, %region_4.6_spmd} | conditional | flops 1098002688 | bytes 49550436 | solution.py:64
  110.5 1.0 constant_dynamic-slice_fusion
  111.5 1.5 fusion.2
  113.0 1.7 fusion.6
  114.8 3.2 %bitcast_add_fusion = f32[256,2,8,128]{3,0,2,1:T(8,128)S(1)} fusion(f32[256,2,8,128]{3,0,2,1:T(8,128)S(1)} %copy-done.1, bf16[512,2,128,1]{0,2,3,1:T(8,128)(2,1)S(1)} %bitcast.54, f32[2,512,256,8]{2,1,3,0:T(8,128)S(1)} %get-tuple-element.228, f32[2,8,256]{2,1,0:T(8,128)S(1)} %get-tuple-element.305, pred[256,512]{0,1:T(8,128)(4,1)S(1)} %broadcast_compare_fusion, ...), kind=kOutput, calls=%fused_computation.10 | convolution fusion | flops 546308096 | bytes 13008896 | tf_op jit(solution)/shard_map/while/body/eval_jaxpr/cond/branch_1_fun/kgts,skd->tkgd/dot_general | solution.py:45
  117.9 1.3 copy-done.2
  119.3 0.6 fusion.23
  121.1 9.0 %conditional.3 = ((f32[2,8,256]{2,1,0:T(8,128)S(1)}, f32[2,8,256]{2,1,0:T(8,128)S(1)}, f32[256,2,8,128]{3,0,2,1:T(8,128)})) conditional(s32[]{:T(128)} %convert_element_type.40, (f32[2,8,256]{2,1,0:T(8,128)S(1)}, f32[2,8,256]{2,1,0:T(8,128)S(1)}, f32[256,2,8,128]{3,0,2,1:T(8,128)}) %tuple.45, (s32[1,512]{1,0:T(1,128)S(1)}, s32[2]{0:T(128)S(1)}, ...), branch_computations={%region_3.3_spmd, %region_4.6_spmd} | conditional | flops 1098002688 | bytes 49550436 | solution.py:64
  121.4 1.0 constant_dynamic-slice_fusion
  122.4 1.5 fusion.2
  123.9 1.7 fusion.6
  125.7 3.2 %bitcast_add_fusion = f32[256,2,8,128]{3,0,2,1:T(8,128)S(1)} fusion(f32[256,2,8,128]{3,0,2,1:T(8,128)S(1)} %copy-done.1, bf16[512,2,128,1]{0,2,3,1:T(8,128)(2,1)S(1)} %bitcast.54, f32[2,512,256,8]{2,1,3,0:T(8,128)S(1)} %get-tuple-element.228, f32[2,8,256]{2,1,0:T(8,128)S(1)} %get-tuple-element.305, pred[256,512]{0,1:T(8,128)(4,1)S(1)} %broadcast_compare_fusion, ...), kind=kOutput, calls=%fused_computation.10 | convolution fusion | flops 546308096 | bytes 13008896 | tf_op jit(solution)/shard_map/while/body/eval_jaxpr/cond/branch_1_fun/kgts,skd->tkgd/dot_general | solution.py:45
  128.8 1.3 copy-done.2
  130.2 0.6 fusion.23
  132.0 9.0 %conditional.3 = ((f32[2,8,256]{2,1,0:T(8,128)S(1)}, f32[2,8,256]{2,1,0:T(8,128)S(1)}, f32[256,2,8,128]{3,0,2,1:T(8,128)})) conditional(s32[]{:T(128)} %convert_element_type.40, (f32[2,8,256]{2,1,0:T(8,128)S(1)}, f32[2,8,256]{2,1,0:T(8,128)S(1)}, f32[256,2,8,128]{3,0,2,1:T(8,128)}) %tuple.45, (s32[1,512]{1,0:T(1,128)S(1)}, s32[2]{0:T(128)S(1)}, ...), branch_computations={%region_3.3_spmd, %region_4.6_spmd} | conditional | flops 1098002688 | bytes 49550436 | solution.py:64
  132.3 1.0 constant_dynamic-slice_fusion
  133.3 1.5 fusion.2
  134.8 1.7 fusion.6
  136.6 3.2 %bitcast_add_fusion = f32[256,2,8,128]{3,0,2,1:T(8,128)S(1)} fusion(f32[256,2,8,128]{3,0,2,1:T(8,128)S(1)} %copy-done.1, bf16[512,2,128,1]{0,2,3,1:T(8,128)(2,1)S(1)} %bitcast.54, f32[2,512,256,8]{2,1,3,0:T(8,128)S(1)} %get-tuple-element.228, f32[2,8,256]{2,1,0:T(8,128)S(1)} %get-tuple-element.305, pred[256,512]{0,1:T(8,128)(4,1)S(1)} %broadcast_compare_fusion, ...), kind=kOutput, calls=%fused_computation.10 | convolution fusion | flops 546308096 | bytes 13008896 | tf_op jit(solution)/shard_map/while/body/eval_jaxpr/cond/branch_1_fun/kgts,skd->tkgd/dot_general | solution.py:45
  139.7 1.3 copy-done.2
  141.1 1.9 %copy.28 = f32[256,2,8,128]{0,3,2,1:T(8,128)S(1)} copy(f32[256,2,8,128]{3,0,2,1:T(8,128)} %get-tuple-element.142) | data formatting | bytes 4194304 | tf_op jit(solution)/shard_map/while | solution.py:77
  143.0 0.2 divide_convert_fusion
  143.2 11.6 %fusion.15 = bf16[4096,256]{0,1:T(8,128)(2,1)} fusion(bf16[256,2048]{0,1:T(8,128)(2,1)S(1)} %bitcast.55, bf16[2048,4096]{1,0:T(8,128)(2,1)} %param.12), kind=kOutput, calls=%fused_computation.22 | convolution fusion | flops 4296015872 | bytes 19922944 | tf_op jit(solution)/shard_map/dot_general | solution.py:82
  154.8 28.6 %reduce-scatter.2.cloned.1.call-done = bf16[1024,256]{0,1:T(8,128)(2,1)} async-done(((bf16[4096,256]{0,1:T(8,128)(2,1)}), bf16[1024,256]{0,1:T(8,128)(2,1)}) %reduce-scatter.2.cloned.1.call-update) | async-done | bytes 524304 | tf_op jit(solution)/shard_map/reduce_scatter | solution.py:81
  (51 shorter events, 1.3 us)
Async XLA Ops:
  6.5 1.0 copy-start
  6.5 46.0 %all-gather.3.cloned.1.call-start = ((), (), s32[]{:S(2)}) async-start(), calls=%async_computation.1 | async-start | bytes 1179648 | tf_op jit(solution)/shard_map/all_gather | solution.py:58
  8.3 85.4 %all-gather.5.cloned.1.call-start = ((), (), s32[]{:S(2)}) async-start(), calls=%async_computation.2 | async-start | bytes 1179648 | tf_op jit(solution)/shard_map/all_gather | solution.py:59
  9.9 173.5 %reduce-scatter.2.cloned.1.call-start = ((), (), s32[]{:S(2)}) async-start(), calls=%async_computation.3 | async-start | bytes 2621440 | tf_op jit(solution)/shard_map/reduce_scatter | solution.py:81
  100.6 3.3 %copy-start.1 = (f32[256,2,8,128]{3,0,2,1:T(8,128)S(1)}, f32[256,2,8,128]{3,0,2,1:T(8,128)}, u32[]{:S(2)}) copy-start(f32[256,2,8,128]{3,0,2,1:T(8,128)} %get-tuple-element.124) | copy-start | bytes 6291460 | tf_op jit(solution)/shard_map/while/body/eval_jaxpr/cond
  107.0 1.3 copy-start.2
  111.5 3.3 %copy-start.1 = (f32[256,2,8,128]{3,0,2,1:T(8,128)S(1)}, f32[256,2,8,128]{3,0,2,1:T(8,128)}, u32[]{:S(2)}) copy-start(f32[256,2,8,128]{3,0,2,1:T(8,128)} %get-tuple-element.124) | copy-start | bytes 6291460 | tf_op jit(solution)/shard_map/while/body/eval_jaxpr/cond
  117.9 1.3 copy-start.2
  122.4 3.3 %copy-start.1 = (f32[256,2,8,128]{3,0,2,1:T(8,128)S(1)}, f32[256,2,8,128]{3,0,2,1:T(8,128)}, u32[]{:S(2)}) copy-start(f32[256,2,8,128]{3,0,2,1:T(8,128)} %get-tuple-element.124) | copy-start | bytes 6291460 | tf_op jit(solution)/shard_map/while/body/eval_jaxpr/cond
  128.8 1.3 copy-start.2
  133.3 3.3 %copy-start.1 = (f32[256,2,8,128]{3,0,2,1:T(8,128)S(1)}, f32[256,2,8,128]{3,0,2,1:T(8,128)}, u32[]{:S(2)}) copy-start(f32[256,2,8,128]{3,0,2,1:T(8,128)} %get-tuple-element.124) | copy-start | bytes 6291460 | tf_op jit(solution)/shard_map/while/body/eval_jaxpr/cond
  139.7 1.3 copy-start.2
Sparse Core Ops, SparseCore 0:
  9.5 43.0 all-gather.2
  54.6 38.9 all-gather.4
  154.9 28.4 reduce-scatter.1
where the time goes:
time: 190 us
  waiting for transfers between devices  91.2 us (48%)
  matrix products  30.2 us (16%)
  local copies, waits for them, and re-layouts  24.3 us (13%)
  between operations  13.9 us (7%)
  blocking collectives  13.1 us (7%)
  other arithmetic  11.9 us (6%)
  loops' own time  5.26 us (3%)
    all_gather x1, waiting for transfers between devices, shards(): piece_values = lax.all_gather(own_values, 'ctx', axis=0, tiled=True)  39.6 us
    reduce_scatter x1, waiting for transfers between devices, shards(): lax.psum_scatter(lax.dot_general(out_weight, attended, (((0,), (1,)), (()...  28.6 us
    all_gather x1, waiting for transfers between devices, shards(): piece_keys = lax.all_gather(own_keys, 'ctx', axis=0, tiled=True)  22.8 us
    unnamed x1, blocking collectives  13.1 us
    dot_general x4, matrix products, update(): jnp.einsum('kgts,skd->tkgd', weights.astype(jnp.bfloat16), valued, prefer...  12.6 us
    dot_general x1, matrix products, shards(): lax.dot_general(out_weight, attended, (((0,), (1,)), ((), ())), preferred...  11.6 us
    unnamed x10, local copies, waits for them, and re-layouts  9.18 us
    reduce_sum x4, other arithmetic, update(): run_sum = run_sum * factor + jnp.sum(weights, axis=-1)  6.79 us
  transfers between devices with their start and end apart: 3, of which 3 were waited for; matrix products, arithmetic and copies ran while one was open for 5% of the time, Pallas kernels for 0%

commit v1 on v0

--- a/solution.py
+++ b/solution.py
@@ -55,8 +55,11 @@
         jnp.zeros((kv_heads, head_group, tok_rows), jnp.float32),
         jnp.zeros((tok_rows, kv_heads, head_group, HEAD_SIZE), jnp.float32),
     )
-    piece_keys = lax.all_gather(own_keys, "ctx", axis=0, tiled=True)
-    piece_values = lax.all_gather(own_values, "ctx", axis=0, tiled=True)
+    piece_keys, piece_values = jnp.split(
+        lax.all_gather(jnp.concatenate([own_keys, own_values], axis=1), "ctx", axis=0, tiled=True),
+        [own_keys.shape[1]],
+        axis=1,
+    )
     rows = piece_keys.shape[0]
     step_rows = math.gcd(rows, 512)
 

time: 190 us -> 157 us (0.83)
  waiting for transfers between devices: 91.2 us -> 63.2 us
  local copies, waits for them, and re-layouts: 24.3 us -> 16.2 us
  other arithmetic: 11.9 us -> 14.2 us
    all_gather x2 -> x1, waiting for transfers between devices: 62.5 us -> 33.4 us  [shards(): lax.all_gather(jnp.concatenate([own_keys, own_values], axis=1), 'ctx', ax...]
    cond x20 -> x4, local copies, waits for them, and re-layouts: 5.35 us -> 0.01 us
    unnamed x10 -> x8, local copies, waits for them, and re-layouts: 9.18 us -> 7.02 us
  transfers between devices with their start and end apart: 3 -> 2, of which waited for: 3 -> 2; matrix products, arithmetic and copies ran while one was open for 5% -> 4% of each run, Pallas kernels for 0% -> 0%
where the time goes in v1:
time: 157 us
  waiting for transfers between devices  63.2 us (40%)
  matrix products  30.3 us (19%)
  local copies, waits for them, and re-layouts  16.2 us (10%)
  other arithmetic  14.2 us (9%)
  between operations  14.1 us (9%)
  blocking collectives  13.2 us (8%)
  loops' own time  5.42 us (3%)
    all_gather x1, waiting for transfers between devices, shards(): lax.all_gather(jnp.concatenate([own_keys, own_values], axis=1), 'ctx', ax...  33.4 us
    reduce_scatter x1, waiting for transfers between devices, shards(): lax.psum_scatter(lax.dot_general(out_weight, attended, (((0,), (1,)), (()...  29.8 us
    unnamed x1, blocking collectives  13.2 us
    dot_general x4, matrix products, update(): jnp.einsum('kgts,skd->tkgd', weights.astype(jnp.bfloat16), valued, prefer...  12.6 us
    dot_general x1, matrix products, shards(): lax.dot_general(out_weight, attended, (((0,), (1,)), ((), ())), preferred...  11.6 us
    unnamed x8, local copies, waits for them, and re-layouts  7.02 us
    reduce_sum x4, other arithmetic, update(): run_sum = run_sum * factor + jnp.sum(weights, axis=-1)  6.79 us
    dot_general x4, matrix products, update(): jnp.einsum('tkgd,skd->kgts', query_heads, keyed, preferred_element_type=j...  6.08 us
  transfers between devices with their start and end apart: 2, of which 2 were waited for; matrix products, arithmetic and copies ran while one was open for 4% of the time, Pallas kernels for 0%

profile of v1, /device:TPU:0, one launch (start us, length us, event | category | flops | bytes accessed | tf_op | source)
XLA Modules:
  0.0 156.6 jit_solution(16424390175941767919)
XLA Ops:
  6.5 1.0 constant_dynamic-slice_fusion.3
  7.5 0.7 pad_maximum_fusion
  8.3 1.3 dynamic-slice
  10.2 0.9 dynamic-update-slice
  11.1 13.2 %all-reduce = s32[16]{0:T(128)S(1)} all-reduce(s32[16]{0:T(128)S(1)} %dynamic-update-slice), channel_id=1, replica_groups=mesh['ctx'=8,'tp'=4] {'ctx'}, use_global_device_ids=true, to_apply=%add | all-reduce | flops 16 | bytes 128
  24.3 0.1 add.57
  24.4 1.5 copy.24
  25.8 0.7 copy.26
  26.5 0.7 broadcast_multiply_fusion
  27.2 0.7 add_reduce_fusion
  28.0 33.4 %all-gather.2.cloned.1.call-done = bf16[2048,512]{1,0:T(8,128)(2,1)} async-done(((bf16[256,512]{1,0:T(8,128)(2,1)}), bf16[2048,512]{1,0:T(8,128)(2,1)}) %all-gather.2.cloned.1.call-update) | async-done | bytes 2097168 | tf_op jit(solution)/shard_map/all_gather | solution.py:59
  61.4 1.7 %fusion.17 = (bf16[2048,256]{1,0:T(8,128)(2,1)S(1)}, bf16[2048,256]{1,0:T(8,128)(2,1)S(1)}) fusion(bf16[2048,512]{1,0:T(8,128)(2,1)} %all-gather.2.cloned.1.call-done), kind=kLoop, calls=%fused_computation.34 | loop fusion | bytes 4194304 | tf_op jit(solution)/shard_map/split | solution.py:58
  63.0 1.3 copy.25
  64.4 1.3 copy.27
  65.7 0.2 broadcast_in_dim.44
  65.9 38.7 %while.15 = (s32[]{:T(128)}, f32[2,8,256]{2,1,0:T(8,128)S(1)}, f32[2,8,256]{2,1,0:T(8,128)S(1)}, f32[256,2,8,128]{3,0,2,1:T(8,128)S(1)}, s32[4,512]{1,0:T(4,128)...) while((s32[]{:T(128)}, f32[2,8,256]{2,1,0:T(8,128)S(1)}, ...), condition=%wide.region_7.8_spmd.clone, body=%wide.region_1.7_spmd.clone.sunk | while | flops 1098003200 | bytes 32778520 | solution.py:80
  65.9 0.6 fusion.24
  67.8 7.7 %conditional.3 = ((f32[2,8,256]{2,1,0:T(8,128)S(1)}, f32[2,8,256]{2,1,0:T(8,128)S(1)}, f32[256,2,8,128]{3,0,2,1:T(8,128)S(1)})) conditional(s32[]{:T(128)} %convert_element_type.40, (f32[2,8,256]{2,1,0:T(8,128)S(1)}, f32[2,8,256]{2,1,0:T(8,128)S(1)}, f32[256,2,8,128]{3,0,2,1:T(8,128)S(1)}) %tuple.47, (s32[1,512]{1,0:T(1,128)S(1)}, s32[2]{0:T(128)S(1)}, ...), branch_computations={%region_3.3_spmd, %region_4.6_spmd} | conditional | flops 1098002688 | bytes 32773164 | solution.py:67
  67.9 0.1 broadcast_compare_fusion
  68.1 1.1 constant_dynamic-slice_fusion
  69.2 1.5 fusion.2
  70.7 1.7 %fusion.6 = f32[2,8,256]{2,1,0:T(8,128)S(1)} fusion(f32[2,512,256,8]{2,1,3,0:T(8,128)S(1)} %get-tuple-element.228, f32[2,8,256]{2,1,0:T(8,128)S(1)} %get-tuple-element.309, pred[256,512]{0,1:T(8,128)(4,1)S(1)} %broadcast_compare_fusion), kind=kLoop, calls=%fused_computation.7 | loop fusion | flops 8384512 | bytes 8552448 | tf_op jit(solution)/shard_map/while/body/eval_jaxpr/cond/branch_1_fun/reduce_sum | solution.py:43
  72.4 3.2 %bitcast_add_fusion = f32[256,2,8,128]{3,0,2,1:T(8,128)S(1)} fusion(f32[256,2,8,128]{3,0,2,1:T(8,128)S(1)} %get-tuple-element.124, bf16[512,2,128,1]{0,2,3,1:T(8,128)(2,1)S(1)} %bitcast.54, f32[2,512,256,8]{2,1,3,0:T(8,128)S(1)} %get-tuple-element.228, f32[2,8,256]{2,1,0:T(8,128)S(1)} %get-tuple-element.309, ...), kind=kOutput, calls=%fused_computation.10 | convolution fusion | flops 546308096 | bytes 13008896 | tf_op jit(solution)/shard_map/while/body/eval_jaxpr/cond/branch_1_fun/kgts,skd->tkgd/dot_general | solution.py:45
  75.6 0.6 fusion.24
  77.5 7.7 %conditional.3 = ((f32[2,8,256]{2,1,0:T(8,128)S(1)}, f32[2,8,256]{2,1,0:T(8,128)S(1)}, f32[256,2,8,128]{3,0,2,1:T(8,128)S(1)})) conditional(s32[]{:T(128)} %convert_element_type.40, (f32[2,8,256]{2,1,0:T(8,128)S(1)}, f32[2,8,256]{2,1,0:T(8,128)S(1)}, f32[256,2,8,128]{3,0,2,1:T(8,128)S(1)}) %tuple.47, (s32[1,512]{1,0:T(1,128)S(1)}, s32[2]{0:T(128)S(1)}, ...), branch_computations={%region_3.3_spmd, %region_4.6_spmd} | conditional | flops 1098002688 | bytes 32773164 | solution.py:67
  77.6 0.1 broadcast_compare_fusion
  77.8 1.1 constant_dynamic-slice_fusion
  78.8 1.5 fusion.2
  80.4 1.7 %fusion.6 = f32[2,8,256]{2,1,0:T(8,128)S(1)} fusion(f32[2,512,256,8]{2,1,3,0:T(8,128)S(1)} %get-tuple-element.228, f32[2,8,256]{2,1,0:T(8,128)S(1)} %get-tuple-element.309, pred[256,512]{0,1:T(8,128)(4,1)S(1)} %broadcast_compare_fusion), kind=kLoop, calls=%fused_computation.7 | loop fusion | flops 8384512 | bytes 8552448 | tf_op jit(solution)/shard_map/while/body/eval_jaxpr/cond/branch_1_fun/reduce_sum | solution.py:43
  82.1 3.2 %bitcast_add_fusion = f32[256,2,8,128]{3,0,2,1:T(8,128)S(1)} fusion(f32[256,2,8,128]{3,0,2,1:T(8,128)S(1)} %get-tuple-element.124, bf16[512,2,128,1]{0,2,3,1:T(8,128)(2,1)S(1)} %bitcast.54, f32[2,512,256,8]{2,1,3,0:T(8,128)S(1)} %get-tuple-element.228, f32[2,8,256]{2,1,0:T(8,128)S(1)} %get-tuple-element.309, ...), kind=kOutput, calls=%fused_computation.10 | convolution fusion | flops 546308096 | bytes 13008896 | tf_op jit(solution)/shard_map/while/body/eval_jaxpr/cond/branch_1_fun/kgts,skd->tkgd/dot_general | solution.py:45
  85.3 0.6 fusion.24
  87.2 7.7 %conditional.3 = ((f32[2,8,256]{2,1,0:T(8,128)S(1)}, f32[2,8,256]{2,1,0:T(8,128)S(1)}, f32[256,2,8,128]{3,0,2,1:T(8,128)S(1)})) conditional(s32[]{:T(128)} %convert_element_type.40, (f32[2,8,256]{2,1,0:T(8,128)S(1)}, f32[2,8,256]{2,1,0:T(8,128)S(1)}, f32[256,2,8,128]{3,0,2,1:T(8,128)S(1)}) %tuple.47, (s32[1,512]{1,0:T(1,128)S(1)}, s32[2]{0:T(128)S(1)}, ...), branch_computations={%region_3.3_spmd, %region_4.6_spmd} | conditional | flops 1098002688 | bytes 32773164 | solution.py:67
  87.3 0.1 broadcast_compare_fusion
  87.4 1.1 constant_dynamic-slice_fusion
  88.5 1.5 fusion.2
  90.1 1.7 %fusion.6 = f32[2,8,256]{2,1,0:T(8,128)S(1)} fusion(f32[2,512,256,8]{2,1,3,0:T(8,128)S(1)} %get-tuple-element.228, f32[2,8,256]{2,1,0:T(8,128)S(1)} %get-tuple-element.309, pred[256,512]{0,1:T(8,128)(4,1)S(1)} %broadcast_compare_fusion), kind=kLoop, calls=%fused_computation.7 | loop fusion | flops 8384512 | bytes 8552448 | tf_op jit(solution)/shard_map/while/body/eval_jaxpr/cond/branch_1_fun/reduce_sum | solution.py:43
  91.8 3.2 %bitcast_add_fusion = f32[256,2,8,128]{3,0,2,1:T(8,128)S(1)} fusion(f32[256,2,8,128]{3,0,2,1:T(8,128)S(1)} %get-tuple-element.124, bf16[512,2,128,1]{0,2,3,1:T(8,128)(2,1)S(1)} %bitcast.54, f32[2,512,256,8]{2,1,3,0:T(8,128)S(1)} %get-tuple-element.228, f32[2,8,256]{2,1,0:T(8,128)S(1)} %get-tuple-element.309, ...), kind=kOutput, calls=%fused_computation.10 | convolution fusion | flops 546308096 | bytes 13008896 | tf_op jit(solution)/shard_map/while/body/eval_jaxpr/cond/branch_1_fun/kgts,skd->tkgd/dot_general | solution.py:45
  95.0 0.6 fusion.24
  96.9 7.7 %conditional.3 = ((f32[2,8,256]{2,1,0:T(8,128)S(1)}, f32[2,8,256]{2,1,0:T(8,128)S(1)}, f32[256,2,8,128]{3,0,2,1:T(8,128)S(1)})) conditional(s32[]{:T(128)} %convert_element_type.40, (f32[2,8,256]{2,1,0:T(8,128)S(1)}, f32[2,8,256]{2,1,0:T(8,128)S(1)}, f32[256,2,8,128]{3,0,2,1:T(8,128)S(1)}) %tuple.47, (s32[1,512]{1,0:T(1,128)S(1)}, s32[2]{0:T(128)S(1)}, ...), branch_computations={%region_3.3_spmd, %region_4.6_spmd} | conditional | flops 1098002688 | bytes 32773164 | solution.py:67
  97.0 0.1 broadcast_compare_fusion
  97.1 1.1 constant_dynamic-slice_fusion
  98.2 1.5 fusion.2
  99.7 1.7 %fusion.6 = f32[2,8,256]{2,1,0:T(8,128)S(1)} fusion(f32[2,512,256,8]{2,1,3,0:T(8,128)S(1)} %get-tuple-element.228, f32[2,8,256]{2,1,0:T(8,128)S(1)} %get-tuple-element.309, pred[256,512]{0,1:T(8,128)(4,1)S(1)} %broadcast_compare_fusion), kind=kLoop, calls=%fused_computation.7 | loop fusion | flops 8384512 | bytes 8552448 | tf_op jit(solution)/shard_map/while/body/eval_jaxpr/cond/branch_1_fun/reduce_sum | solution.py:43
  101.5 3.2 %bitcast_add_fusion = f32[256,2,8,128]{3,0,2,1:T(8,128)S(1)} fusion(f32[256,2,8,128]{3,0,2,1:T(8,128)S(1)} %get-tuple-element.124, bf16[512,2,128,1]{0,2,3,1:T(8,128)(2,1)S(1)} %bitcast.54, f32[2,512,256,8]{2,1,3,0:T(8,128)S(1)} %get-tuple-element.228, f32[2,8,256]{2,1,0:T(8,128)S(1)} %get-tuple-element.309, ...), kind=kOutput, calls=%fused_computation.10 | convolution fusion | flops 546308096 | bytes 13008896 | tf_op jit(solution)/shard_map/while/body/eval_jaxpr/cond/branch_1_fun/kgts,skd->tkgd/dot_general | solution.py:45
  104.6 1.9 %copy.28 = f32[256,2,8,128]{0,3,2,1:T(8,128)} copy(f32[256,2,8,128]{3,0,2,1:T(8,128)S(1)} %get-tuple-element.142) | data formatting | bytes 4194304 | tf_op jit(solution)/shard_map/while | solution.py:80
  106.5 1.8 %divide_convert_fusion = bf16[256,2,8,128]{0,3,2,1:T(8,128)(2,1)S(1)} fusion(f32[256,2,8,128]{0,3,2,1:T(8,128)} %copy.28, f32[256,2,8]{0,2,1:T(8,128)S(1)} %bitcast.59), kind=kLoop, calls=%fused_computation.23 | loop fusion | flops 1048576 | bytes 3162112 | tf_op jit(solution)/shard_map/convert_element_type | solution.py:83
  108.3 11.6 %fusion.15 = bf16[4096,256]{0,1:T(8,128)(2,1)} fusion(bf16[256,2048]{0,1:T(8,128)(2,1)S(1)} %bitcast.55, bf16[2048,4096]{1,0:T(8,128)(2,1)} %param.12), kind=kOutput, calls=%fused_computation.22 | convolution fusion | flops 4296015872 | bytes 19922944 | tf_op jit(solution)/shard_map/dot_general | solution.py:85
  119.9 29.8 %reduce-scatter.2.cloned.1.call-done = bf16[1024,256]{0,1:T(8,128)(2,1)} async-done(((bf16[4096,256]{0,1:T(8,128)(2,1)}), bf16[1024,256]{0,1:T(8,128)(2,1)}) %reduce-scatter.2.cloned.1.call-update) | async-done | bytes 524304 | tf_op jit(solution)/shard_map/reduce_scatter | solution.py:84
  (31 shorter events, 0.6 us)
Async XLA Ops:
  6.5 54.8 %all-gather.2.cloned.1.call-start = ((), (), s32[]{:S(2)}) async-start(), calls=%async_computation.1 | async-start | bytes 2359296 | tf_op jit(solution)/shard_map/all_gather | solution.py:59
  8.3 141.5 %reduce-scatter.2.cloned.1.call-start = ((), (), s32[]{:S(2)}) async-start(), calls=%async_computation.2 | async-start | bytes 2621440 | tf_op jit(solution)/shard_map/reduce_scatter | solution.py:84
Sparse Core Ops, SparseCore 0:
  9.5 51.8 all-gather.1
  120.1 29.6 reduce-scatter.1
